TPU v7x, 32 devices: a whole 2x2x4 slice. The times are simulated.
32 devices in a mesh: tile: 4 (over x, core), chan: 4 (over z), beam: 2 (over y).
Axes of the slice: x: 2, y: 2, z: 4, core: 2. Of those that a mesh axis runs over, the one named last changes fastest.
Arguments:
- voltages: bfloat16 [32, 128, 2, 2, 1536], P(None, 'tile', None, None, 'chan'), may hold values from -6 to 6
- calib_gain: float32 [128, 2, 2, 1536], P(('tile', 'beam'), None, None, 'chan'), may hold values from -0.375 to 0.375
- tile_flags: int32 [128], P(('tile', 'beam')), may hold values 0 or 1
- delays: float32 [64, 128], P(None, 'tile'), may hold values from -4 to 4
- pointing: int32 [2], P('beam'), may hold values from 0 to 63
- synth_filter: float32 [12, 128], replicated, may hold values from -0.5 to 0.5
Outputs:
- streams: float32 [32, 2, 2, 12, 256], P('tile', 'beam', None, 'chan')
Inputs may be any that keep to these rules, and one draw needn't show every extreme that they name: `tile_flags`: 1 marks a tile in use. `pointing`: a row of delays, one of 64.
All inputs are finite; a program needn't handle non-finite values. No bound on the sum of `tile_flags` on one device may be relied on, other than what follows from the above.
Results may differ from a plain program's by a relative error of at most 0.0003.
Values sent between devices are 32-bit elements; how exact they have to be, the bound alone decides.
A program may use at most 64 MiB of HBM per device.

v0:
```python
import math

import jax
import jax.numpy as jnp
from jax import lax
from jax.sharding import PartitionSpec as P

K = 128
COARSE = 12


TWO_PI = 6.283185307179586
HIGHEST = lax.Precision.HIGHEST


def channel_frequency(first_index, length):
    global_idx = first_index + jnp.arange(length, dtype=jnp.int32)
    physical = global_idx % COARSE * K + global_idx // COARSE
    return (physical.astype(jnp.float32) + 0.5) / (K * COARSE)


def beam_weights(calib_gain, tile_flags, tile_delay, frequency):
    phase_angle = (TWO_PI * tile_delay)[:, :, None] * frequency[None, None, :]
    cosine = jnp.cos(phase_angle)[:, :, None, :]
    sine_part = jnp.sin(phase_angle)[:, :, None, :]
    gain_re = calib_gain[:, :, 0, :][None]
    gain_im = calib_gain[:, :, 1, :][None]
    in_use = tile_flags[None, :, None, None]
    weight_re = in_use * (gain_re * cosine + gain_im * sine_part)
    weight_im = in_use * (gain_im * cosine - gain_re * sine_part)
    return (weight_re, weight_im)


def inverse_table():
    ordinal = jnp.arange(K, dtype=jnp.int32)
    residue = ordinal[:, None] * ordinal[None, :] % K
    radians = TWO_PI * residue.astype(jnp.float32) / K
    cosine = jnp.cos(radians) / math.sqrt(K)
    sine_part = jnp.sin(radians) / math.sqrt(K)
    from_real = jnp.concatenate([cosine, sine_part], axis=1)
    from_imag = jnp.concatenate([-sine_part, cosine], axis=1)
    return jnp.stack([from_real, from_imag], axis=0)


def transform(grouped, table):
    return jnp.einsum(
        "tbprfc,rfm->tbpcm", grouped, table, precision=HIGHEST, preferred_element_type=jnp.float32
    )


def synthesize(extended, synth_filter, row_count):
    tap_count = synth_filter.shape[0]
    doubled = jnp.concatenate([synth_filter, synth_filter], axis=1)
    total = jnp.zeros((row_count,) + extended.shape[1:], jnp.float32)
    for offset in range(tap_count):
        begin = tap_count - 1 - offset
        total = total + doubled[offset] * extended[begin : begin + row_count]
    return total


def body(voltages, calib_gain, tile_flags, delays, pointing, synth_filter):
    gains_all, flags_all = (
        lax.all_gather(calib_gain, "beam", axis=0, tiled=True),
        lax.all_gather(tile_flags.astype(jnp.float32), "beam", axis=0, tiled=True),
    )
    local_len = calib_gain.shape[-1]
    frequency = channel_frequency(lax.axis_index("chan") * local_len, local_len)
    table_rows = delays.shape[0]
    onehot = (jnp.arange(table_rows, dtype=jnp.int32)[None, :] == pointing[:, None]).astype(
        jnp.float32
    )
    tile_delay = jnp.dot(onehot, delays, precision=HIGHEST, preferred_element_type=jnp.float32)
    weight_re, weight_im = beam_weights(gains_all, flags_all, tile_delay, frequency)
    total_rows = voltages.shape[0]
    fine_local = local_len // COARSE
    table = inverse_table()
    lag_rows = synth_filter.shape[0] - 1
    block = voltages.astype(jnp.float32)
    volt_re = block[:, None, :, :, 0, :]
    volt_im = block[:, None, :, :, 1, :]
    beam_re = jnp.sum(weight_re[None] * volt_re - weight_im[None] * volt_im, axis=2)
    beam_im = jnp.sum(weight_re[None] * volt_im + weight_im[None] * volt_re, axis=2)
    partial_value = jnp.stack([beam_re, beam_im], axis=3)
    grouped = lax.all_to_all(
        partial_value.reshape(partial_value.shape[:4] + (fine_local, COARSE)),
        "chan",
        split_axis=5,
        concat_axis=4,
        tiled=True,
    )
    spectra = transform(grouped, table)
    leading = jnp.zeros((lag_rows,) + spectra.shape[1:], jnp.float32)
    padded = jnp.concatenate([leading, spectra], axis=0)
    streams = synthesize(padded, synth_filter, total_rows)
    return lax.psum_scatter(streams, "tile", scatter_dimension=0, tiled=True)


def solution(mesh):
    in_specs = (
        P(None, "tile", None, None, "chan"),
        P(("tile", "beam"), None, None, "chan"),
        P(("tile", "beam")),
        P(None, "tile"),
        P("beam"),
        P(),
    )
    out_specs = P("tile", "beam", None, "chan", None)
    return jax.shard_map(body, mesh=mesh, in_specs=in_specs, out_specs=out_specs, check_vma=False)
```

profile of v0, /device:TPU:1, one launch (start us, length us, event | category | flops | bytes accessed | tf_op | source)
XLA Modules:
  0.0 83.6 jit_solution(12575908222803293127)
XLA Ops:
  7.2 1.3 %dynamic-slice = u32[1]{0:T(128)} dynamic-slice(u32[32]{0:T(128)} %constant.67, u32[]{:T(128)S(6)} %add.131), dynamic_slice_sizes={1} | dynamic-slice | bytes 12
  9.2 0.8 convert_dynamic-update-slice_fusion
  10.0 4.3 %all-reduce.1 = f32[32]{0:T(128)S(1)} all-reduce(f32[32]{0:T(128)S(1)} %convert_dynamic-update-slice_fusion), channel_id=1, replica_groups=mesh['tile'=4,'chan'=4,'beam'=2] {'beam'}, use_global_device_ids=true, to_apply=%add.1 | all-reduce | flops 32 | bytes 256
  14.3 0.9 %copy.15 = f32[16,2,2,384]{3,0,1,2:T(8,128)S(1)} copy(f32[16,2,2,384]{3,2,1,0:T(2,128)} %param.7) | data formatting | bytes 196608 | tf_op args[1]
  15.2 4.1 %all_gather.7 = f32[32,2,2,384]{3,0,1,2:T(8,128)S(1)} all-gather(f32[16,2,2,384]{3,0,1,2:T(8,128)S(1)} %copy.15), channel_id=1, replica_groups=mesh['tile'=4,'chan'=4,'beam'=2] {'beam'}, dimensions={0}, use_global_device_ids=true | all-gather | bytes 294912 | tf_op jit(solution)/shard_map/all_gather | solution.py:63
  19.4 0.1 fusion
  19.5 0.3 multiply_cosine_fusion
  19.8 0.1 add_multiply_fusion
  19.9 0.1 copy.16
  19.9 0.1 copy.17
  20.0 4.5 %convert_element_type.25 = f32[32,32,2,2,384]{4,3,2,1,0:T(2,128)S(1)} convert(bf16[32,32,2,2,384]{4,3,2,1,0:T(2,128)(2,1)} %param.6) | non-fusion elementwise | flops 1572864 | bytes 9437184 | tf_op jit(solution)/shard_map/convert_element_type | solution.py:78
  24.6 10.5 %subtract_reduce_fusion = (f32[32,2,384]{2,1,0:T(2,128)S(1)}, f32[32,2,384]{2,1,0:T(2,128)S(1)}) fusion(f32[32,32,2,2,384]{4,3,2,1,0:T(2,128)S(1)} %convert_element_type.25, f32[32,2,384]{2,1,0:T(2,128)S(1)} %copy.17, f32[32,2,384]{2,1,0:T(2,128)S(1)} %copy.16), kind=kLoop, calls=%fused_computation.3 | loop fusion | flops 6242304 | bytes 6684672 | tf_op jit(solution)/shard_map/reduce_sum | solution.py:81
  35.1 0.0 copy-start.1
  35.1 0.2 copy.19
  35.3 0.2 copy.18
  35.5 0.5 copy_bitcast_fusion
  36.0 1.5 %reshape.261 = f32[4,1,12288]{2,1,0:T(1,128)} reshape(f32[12,1,2,32,2,32]{5,4,3,2,1,0:T(2,128)S(1)} %copy_bitcast_fusion) | data formatting | bytes 393216
  37.4 4.8 %all-to-all-start = ((f32[4,1,12288]{2,1,0:T(1,128)}), f32[4,1,12288]{2,1,0:T(1,128)S(1)}, u32[]{:S(2)}, u32[]{:S(2)}) async-start(f32[4,1,12288]{2,1,0:T(1,128)} %reshape.261), calls=%async_computation | async-start | bytes 393216 | tf_op jit(solution)/shard_map/all_to_all | solution.py:84
  42.3 0.3 sine_multiply_fusion
  42.5 0.3 fusion.32
  42.9 4.5 %all-to-all-done = f32[4,1,12288]{2,1,0:T(1,128)S(1)} async-done(((f32[4,1,12288]{2,1,0:T(1,128)}), f32[4,1,12288]{2,1,0:T(1,128)S(1)}, u32[]{:S(2)}, u32[]{:S(2)}) %all-to-all-start) | async-done | bytes 196640 | tf_op jit(solution)/shard_map/all_to_all | solution.py:84
  47.4 0.5 broadcast.215
  47.9 1.2 %reduce.2 = f32[4,12288]{1,0:T(4,128)S(1)} reduce(f32[4,1,12288]{2,1,0:T(1,128)S(1)} %all-to-all-done, f32[]{:T(128)} %broadcast.215), dimensions={1}, to_apply=%all_to_all.11.reduce_sub_computation | reduce | bytes 393220 | tf_op jit(solution)/shard_map/all_to_all | solution.py:84
  49.0 0.7 reshape.262
  49.7 0.4 copy.21
  50.2 0.5 copy.22
  50.7 0.4 reshape.251
  51.1 0.3 fusion.1
  51.4 0.9 %fusion.15 = f32[32,1,2,3,256]{4,0,3,2,1:T(8,128)} fusion(f32[32,1,2,3,256]{4,0,3,2,1:T(8,128)S(1)} %bitcast.77, f32[32,2,3,256,1]{3,0,4,2,1:T(8,128)S(1)} %fusion.1, f32[256]{0:T(256)S(1)} %bitcast.81, f32[256]{0:T(256)S(1)} %bitcast.82, f32[256]{0:T(256)S(1)} %bitcast.83, f32[256]{0:T(256)S(1)} %bitcast.84, f32[256]{0:T(256)S(1)} %bitcast.85, ...), kind=kLoop, calls=%fused_computation.33 | loop fusion | flops 1130496 | bytes 602112 | tf_op jit(solution)/shard_map/add | solution.py:57
  52.3 0.0 reduce-scatter.2.cloned.1.call-update
  52.4 22.9 %reduce-scatter.2.cloned.1.call-done = f32[8,1,2,3,256]{4,0,3,2,1:T(8,128)} async-done(((f32[32,1,2,3,256]{4,0,3,2,1:T(8,128)}), f32[8,1,2,3,256]{4,0,3,2,1:T(8,128)}) %reduce-scatter.2.cloned.1.call-update) | async-done | bytes 49168 | tf_op jit(solution)/shard_map/reduce_scatter | solution.py:95
  75.3 1.4 %copy.23 = f32[8,1,2,3,256]{4,2,3,1,0:T(2,128)} copy(f32[8,1,2,3,256]{4,0,3,2,1:T(8,128)} %reduce-scatter.2.cloned.1.call-done) | data formatting | bytes 98304 | tf_op jit(solution)/shard_map/reduce_scatter | solution.py:95
  (10 shorter events, 0.1 us)
Async XLA Ops:
  6.5 12.8 %copy-start = (f32[64,32]{0,1:T(8,128)S(1)}, f32[64,32]{0,1:T(8,128)}, u32[]{:S(2)}) copy-start(f32[64,32]{0,1:T(8,128)} %param.9) | copy-start | bytes 24580
  35.1 7.7 %copy-start.1 = (f32[12,128]{1,0:T(8,128)S(1)}, f32[12,128]{1,0:T(8,128)}, u32[]{:S(2)}) copy-start(f32[12,128]{1,0:T(8,128)} %param.11) | copy-start | bytes 18436
  37.4 9.9 %all-to-all-start = ((f32[4,1,12288]{2,1,0:T(1,128)}), f32[4,1,12288]{2,1,0:T(1,128)S(1)}, u32[]{:S(2)}, u32[]{:S(2)}) async-start(f32[4,1,12288]{2,1,0:T(1,128)} %reshape.261), calls=%async_computation | async-start | bytes 393216 | tf_op jit(solution)/shard_map/all_to_all | solution.py:84
  42.2 33.1 %reduce-scatter.2.cloned.1.call-start = ((), (), s32[]{:S(2)}) async-start(), calls=%async_computation.2 | async-start | bytes 245760 | tf_op jit(solution)/shard_map/reduce_scatter | solution.py:95
Sparse Core Ops, SparseCore 0:
  52.5 22.7 reduce-scatter.1
where the time goes:
time: 85 us; the launch traced here: 83.6 us
  waiting for transfers between devices  27.4 us (32%)
  other arithmetic  19.3 us (23%)
  between operations  14.9 us (18%)
  blocking collectives  8.47 us (10%)
  local copies, waits for them, and re-layouts  8.27 us (10%)
  starting transfers between devices  4.81 us (6%)
    reduce_scatter x1, waiting for transfers between devices, body(): return lax.psum_scatter(streams, 'tile', scatter_dimension=0, tiled=True)  22.9 us
    reduce_sum x1, other arithmetic, body(): jnp.sum(weight_re[None] * volt_re - weight_im[None] * volt_im, axis=2)  10.5 us
    all_to_all x1, starting transfers between devices, body(): lax.all_to_all(partial_value.reshape(partial_value.shape[:4] + (fine_loca...  4.81 us
    convert_element_type x1, other arithmetic, body(): block = voltages.astype(jnp.float32)  4.52 us
    all_to_all x1, waiting for transfers between devices, body(): lax.all_to_all(partial_value.reshape(partial_value.shape[:4] + (fine_loca...  4.47 us
    unnamed x10, local copies, waits for them, and re-layouts  4.4 us
    unnamed x1, blocking collectives  4.34 us
    all_gather x1, blocking collectives, body(): lax.all_gather(calib_gain, 'beam', axis=0, tiled=True)  4.12 us
  transfers between devices with their start and end apart: 2, of which 2 were waited for; matrix products, arithmetic and copies ran while one was open for 1% of the time, Pallas kernels for 0%

commit v1 on v0

v1 whole, which is shorter than its diff:
```python
import functools
import math

import jax
import jax.numpy as jnp
import numpy as np
from jax import lax
from jax.experimental import pallas as pl
from jax.experimental.pallas import tpu as pltpu
from jax.sharding import PartitionSpec as P

COARSE = 12
LANES = 128
MESH = pl.DeviceIdType.MESH
F32 = jnp.float32
BF16 = jnp.bfloat16


def even_fit(func, degree):
    series = np.polynomial.chebyshev.Chebyshev.interpolate(
        lambda u: func(np.sqrt(u)), degree, domain=[0.0, 0.25]
    )
    return [float(v) for v in series.convert(kind=np.polynomial.Polynomial).coef]


COS_COEF = even_fit(lambda r: np.cos(2 * np.pi * r), 7)
SIN_COEF = even_fit(lambda r: 2 * np.pi * np.sinc(2 * r), 7)


def horner(coef, u):
    total = jnp.full_like(u, coef[-1])
    for value in coef[-2::-1]:
        total = total * u + value
    return total


def split_bf16(table):
    high = table.astype(BF16)
    low = (table - high.astype(np.float64)).astype(BF16)
    return high, low


def dft_table(nz, fz):
    k = nz * fz
    f = np.arange(k)
    m = np.arange(k)
    angle = 2 * np.pi * (f[:, None] * m[None, :] % k) / k
    cosine, sine = np.cos(angle) / math.sqrt(k), np.sin(angle) / math.sqrt(k)
    out = np.zeros((nz, 2, 2, fz, 2, 2, k))
    for p in range(2):
        out[:, p, 0, :, p, 0] = cosine.reshape(nz, fz, k)
        out[:, p, 0, :, p, 1] = sine.reshape(nz, fz, k)
        out[:, p, 1, :, p, 0] = -sine.reshape(nz, fz, k)
        out[:, p, 1, :, p, 1] = cosine.reshape(nz, fz, k)
    return split_bf16(out.reshape(nz * 4 * fz, 4 * k))


def gather_table(nz, fz, cz):
    width = fz * COARSE
    out = np.zeros((width, width), np.float64)
    for c in range(cz):
        for z in range(nz):
            for f in range(fz):
                out[f * COARSE + z * cz + c, (c * nz + z) * fz + f] = 1.0
    return out.astype(BF16)


def kernel(
    cfg,
    volt_ref,
    gain_ref,
    flag_ref,
    delay_ref,
    point_ref,
    synth_ref,
    chan_ref,
    perm_ref,
    dfth_ref,
    dftl_ref,
    out_ref,
    volt,
    gains,
    w_re,
    w_im,
    acc,
    part,
    recv,
    packed,
    inbox,
    spec,
    dft_h,
    dft_l,
    volt_sem,
    table_sem,
    gain_send,
    gain_recv,
    part_send,
    part_recv,
    pack_send,
    pack_recv,
):
    nt, nz, nb, tb, n_all, taps, fz, cz, halo, exchange = cfg
    tile = lax.axis_index("tile")
    chan = lax.axis_index("chan")
    beam = lax.axis_index("beam")
    rows_t = n_all * 4 * cz
    rows_n = 4 * cz

    def peer(t, z, b):
        return {"tile": t, "chan": z, "beam": b}

    order = sorted(range(1, nt), key=lambda d: abs(2 * d - nt)) + [0]
    loads = []
    for slot, d in enumerate(order):
        block = lax.rem(tile + d, nt)
        loads.append(
            pltpu.make_async_copy(
                volt_ref.at[pl.ds(pl.multiple_of(block * (tb * rows_t), 16), tb * rows_t)],
                volt.at[slot],
                volt_sem.at[slot],
            )
        )
    loads[0].start()

    barrier = pltpu.get_barrier_semaphore()
    count = 0
    for dt in range(nt):
        for dz in range(nz):
            if dt or dz:
                pl.semaphore_signal(
                    barrier,
                    inc=1,
                    device_id=peer(lax.rem(tile + dt, nt), lax.rem(chan + dz, nz), beam),
                    device_id_type=MESH,
                )
                count += 1
    for db in range(1, nb):
        pl.semaphore_signal(
            barrier, inc=1, device_id=peer(tile, chan, lax.rem(beam + db, nb)), device_id_type=MESH
        )
        count += 1

    for load in loads[1:]:
        load.start()
    tables = [
        pltpu.make_async_copy(dfth_ref, dft_h, table_sem.at[0]),
        pltpu.make_async_copy(dftl_ref, dft_l, table_sem.at[1]),
    ]
    for copy in tables:
        copy.start()

    pair = 2 * rows_n
    row = lax.broadcasted_iota(jnp.int32, (pair, LANES), 0)
    first = row < rows_n
    even = lax.rem(row, 2) == 0
    n_own = n_all // nb

    if exchange:
        for i in range(n_own // 2):
            use = jnp.where(
                first, flag_ref[2 * i].astype(F32), flag_ref[2 * i + 1].astype(F32)
            )
            gains[beam, pl.ds(i * pair, pair), :] = use * gain_ref[pl.ds(i * pair, pair), :]

    for h in range(1, halo + 1):

        @pl.when(tile < h)
        def _():
            inbox[h] = jnp.zeros(inbox.shape[1:], F32)

    pl.semaphore_wait(barrier, count)

    gain_copies = []
    if exchange:
        for db in range(1, nb):
            copy = pltpu.make_async_remote_copy(
                src_ref=gains.at[beam],
                dst_ref=gains.at[beam],
                send_sem=gain_send.at[db - 1],
                recv_sem=gain_recv.at[db - 1],
                device_id=peer(tile, chan, lax.rem(beam + db, nb)),
                device_id_type=MESH,
            )
            copy.start()
            gain_copies.append(copy)

    select = lax.broadcasted_iota(jnp.int32, delay_ref.shape, 1) == point_ref[0]
    delay = jnp.sum(jnp.where(select, delay_ref[...], 0.0), axis=1, keepdims=True)
    delay = jnp.broadcast_to(delay, (n_all, LANES))
    frequency = (chan_ref[...] + (chan * fz).astype(F32) + 0.5) / (COARSE * nz * fz)

    def phase(i):
        cycles = (
            jnp.where(
                first,
                jnp.broadcast_to(delay[2 * i : 2 * i + 1], (pair, LANES)),
                jnp.broadcast_to(delay[2 * i + 1 : 2 * i + 2], (pair, LANES)),
            )
            * frequency
        )
        turn = cycles - jnp.floor(cycles + 0.5)
        square = turn * turn
        return horner(COS_COEF, square), turn * horner(SIN_COEF, square)

    for i in range(n_all // 2):
        cosine, sine = phase(i)
        w_re[pl.ds(i * pair, pair), :] = cosine
        w_im[pl.ds(i * pair, pair), :] = sine

    for copy in gain_copies:
        copy.wait_recv()

    for i in range(n_all // 2):
        if exchange:
            owner, inner = divmod(2 * i, n_own)
            gain = gains[owner, pl.ds(inner * rows_n, pair), :]
        else:
            gain = gain_ref[pl.ds(i * pair, pair), :]
        cosine = w_re[pl.ds(i * pair, pair), :]
        sine = w_im[pl.ds(i * pair, pair), :]
        swapped = jnp.where(
            even, pltpu.roll(gain, pair - 1, 0), -pltpu.roll(gain, 1, 0)
        )
        weight = gain * cosine + swapped * sine
        w_re[pl.ds(i * pair, pair), :] = jnp.where(even, weight, pltpu.roll(weight, 1, 0))
        w_im[pl.ds(i * pair, pair), :] = jnp.where(even, pltpu.roll(weight, pair - 1, 0), weight)

    quad = 2 * pair
    unroll = 2
    part_copies = []
    for slot, d in enumerate(order):
        loads[slot].wait()

        def step(s, carry):
            sums = [[jnp.zeros((quad, LANES), F32)] * 2 for _ in range(unroll)]
            for q in range(n_all // 4):
                wr = w_re[pl.ds(q * quad, quad), :]
                wi = w_im[pl.ds(q * quad, quad), :]
                for u in range(unroll):
                    begin = pl.multiple_of((s * unroll + u) * rows_t, 16) + q * quad
                    v = volt[slot, pl.ds(begin, quad), :].astype(F32)
                    sums[u] = [sums[u][0] + wr * v, sums[u][1] + wi * v]
            for u in range(unroll):
                begin = pl.multiple_of((s * unroll + u) * quad, 8)
                for which in range(2):
                    value = sums[u][which]
                    acc[slot % 2, pl.ds(begin + which * pair, pair), :] = value[:pair] + value[pair:]
            return carry

        lax.fori_loop(0, tb // unroll, step, 0)

        def take(which, p, c, ri):
            total = None
            for half in range(2):
                start = which * pair + half * rows_n + (p * cz + c) * 2 + ri
                value = acc[slot % 2, pl.ds(start, tb, stride=quad), :]
                total = value if total is None else total + value
            return total

        for p in range(2):
            for c in range(cz):
                part[slot, p * 2 * cz + c] = take(0, p, c, 0) - take(1, p, c, 1)
                part[slot, (p * 2 + 1) * cz + c] = take(0, p, c, 1) + take(1, p, c, 0)
        if d:
            copy = pltpu.make_async_remote_copy(
                src_ref=part.at[slot],
                dst_ref=recv.at[slot],
                send_sem=part_send.at[slot],
                recv_sem=part_recv.at[slot],
                device_id=peer(lax.rem(tile + d, nt), chan, beam),
                device_id_type=MESH,
            )
            copy.start()
            part_copies.append(copy)

    for copy in part_copies:
        copy.wait_recv()

    def total_of(g, c):
        value = part[nt - 1, g * cz + c]
        for slot in range(nt - 1):
            value = value + recv[slot, g * cz + c]
        return value

    sums = jnp.concatenate(
        [jnp.concatenate([total_of(g, c) for c in range(cz)], axis=1) for g in range(4)], axis=0
    )
    high = sums.astype(BF16)
    low = (sums - high.astype(F32)).astype(BF16)
    table = perm_ref[...]
    moved = jnp.dot(high, table, preferred_element_type=F32) + jnp.dot(
        low, table, preferred_element_type=F32
    )
    group = lax.broadcasted_iota(jnp.int32, (tb, LANES), 1) // fz
    for z in range(nz):
        for c in range(cz):
            total = None
            for g in range(4):
                value = moved[g * tb : (g + 1) * tb, c * LANES : (c + 1) * LANES]
                shift = (g - z) * fz % LANES
                if shift:
                    value = pltpu.roll(value, shift, 1)
                total = value if g == 0 else jnp.where(group == g, value, total)
            packed[z, c] = total

    def pack_copy(h, dz):
        return pltpu.make_async_remote_copy(
            src_ref=packed.at[lax.rem(chan + dz, nz)],
            dst_ref=inbox.at[h, chan],
            send_sem=pack_send.at[h, dz],
            recv_sem=pack_recv.at[h, dz],
            device_id=peer(lax.rem(tile + h, nt), lax.rem(chan + dz, nz), beam),
            device_id_type=MESH,
        )

    spread = sorted(range(nz), key=lambda d: abs(2 * d - nz))
    for h in range(halo + 1):
        for dz in spread:
            if h == 0 and dz == 0:
                continue
            if h == 0:
                pack_copy(h, dz).start()
            else:

                @pl.when(tile + h < nt)
                def _():
                    pack_copy(h, dz).start()

    inbox[0, chan] = packed[chan]

    for copy in tables:
        copy.wait()
    for h in range(halo + 1):
        for dz in range(nz):
            if h == 0 and dz == 0:
                continue
            if h == 0:
                pack_copy(h, dz).wait_recv()
            else:

                @pl.when(tile >= h)
                def _():
                    pack_copy(h, dz).wait_recv()

    lhs = jnp.concatenate(
        [
            jnp.concatenate([inbox[h, z, c] for z in range(nz)], axis=1)
            for c in range(cz)
            for h in range(halo, -1, -1)
        ],
        axis=0,
    )
    high = lhs.astype(BF16)
    low = (lhs - high.astype(F32)).astype(BF16)
    spec[...] = (
        jnp.dot(high, dft_h[...], preferred_element_type=F32)
        + jnp.dot(low, dft_h[...], preferred_element_type=F32)
        + jnp.dot(high, dft_l[...], preferred_element_type=F32)
    )
    span = (halo + 1) * tb
    for c in range(cz):
        for g in range(4):
            total = None
            for k in range(taps):
                value = synth_ref[pl.ds(k, 1), :] * spec[
                    pl.ds(c * span + halo * tb - k, tb), g * LANES : (g + 1) * LANES
                ]
                total = value if total is None else total + value
            out_ref[c, :, g * LANES : (g + 1) * LANES] = total

    for copy in gain_copies:
        copy.wait_send()
    for copy in part_copies:
        copy.wait_send()
    for h in range(halo + 1):
        for dz in range(nz):
            if h == 0 and dz == 0:
                continue
            if h == 0:
                pack_copy(h, dz).wait_send()
            else:

                @pl.when(tile + h < nt)
                def _():
                    pack_copy(h, dz).wait_send()


def rows_of(array):
    lead, width = array.shape[:-2], array.shape[-1]
    split = array.reshape(lead + (2, width // LANES, LANES))
    return jnp.swapaxes(split, -3, -2).reshape(-1, LANES)


def body(mesh, voltages, calib_gain, tile_flags, delays, pointing, synth_filter):
    nt, nz, nb = mesh.shape["tile"], mesh.shape["chan"], mesh.shape["beam"]
    total_rows, n_all = voltages.shape[:2]
    width = voltages.shape[-1]
    taps, k = synth_filter.shape
    tb = total_rows // nt
    fz = width // COARSE
    cz = COARSE // nz
    halo = -(-(taps - 1) // tb)
    n_own = calib_gain.shape[0]
    exchange = n_own % 2 == 0
    gain = calib_gain
    if not exchange:
        gain = gain * tile_flags.astype(F32)[:, None, None, None]
        gain = lax.all_gather(gain, "beam", axis=0, tiled=True)
    rows_n = 4 * cz
    r = np.arange(2 * rows_n)[:, None] % rows_n % (2 * cz) // 2
    local = r * LANES + np.arange(LANES)[None, :]
    channel = (local % COARSE * k + local // COARSE).astype(np.float32)
    dft_h, dft_l = dft_table(nz, fz)
    cfg = (nt, nz, nb, tb, n_all, taps, fz, cz, halo, exchange)
    vmem = pl.BlockSpec(memory_space=pltpu.VMEM)
    smem = pl.BlockSpec(memory_space=pltpu.SMEM)
    anywhere = pl.BlockSpec(memory_space=pl.ANY)
    span = (halo + 1) * tb
    dma = pltpu.SemaphoreType.DMA
    out = pl.pallas_call(
        functools.partial(kernel, cfg),
        out_shape=jax.ShapeDtypeStruct((cz, tb, 4 * k), F32),
        in_specs=[anywhere, vmem, smem, vmem, smem, vmem, vmem, vmem, anywhere, anywhere],
        out_specs=vmem,
        scratch_shapes=[
            pltpu.VMEM((nt, tb * n_all * rows_n, LANES), BF16),
            pltpu.VMEM((nb, n_own * rows_n, LANES), F32),
            pltpu.VMEM((n_all * rows_n, LANES), F32),
            pltpu.VMEM((n_all * rows_n, LANES), F32),
            pltpu.VMEM((2, tb * 4 * rows_n, LANES), F32),
            pltpu.VMEM((nt, 4 * cz, tb, LANES), F32),
            pltpu.VMEM((nt - 1, 4 * cz, tb, LANES), F32),
            pltpu.VMEM((nz, cz, tb, LANES), F32),
            pltpu.VMEM((halo + 1, nz, cz, tb, LANES), F32),
            pltpu.VMEM((cz * span, 4 * k), F32),
            pltpu.VMEM(dft_h.shape, BF16),
            pltpu.VMEM(dft_l.shape, BF16),
            dma((nt,)),
            dma((2,)),
            dma((max(nb - 1, 1),)),
            dma((max(nb - 1, 1),)),
            dma((nt,)),
            dma((nt,)),
            dma((halo + 1, nz)),
            dma((halo + 1, nz)),
        ],
        compiler_params=pltpu.CompilerParams(collective_id=0, has_side_effects=True),
    )(
        rows_of(voltages),
        rows_of(gain),
        tile_flags,
        delays.T,
        pointing,
        synth_filter,
        jnp.asarray(channel),
        jnp.asarray(gather_table(nz, fz, cz)),
        jnp.asarray(dft_h),
        jnp.asarray(dft_l),
    )
    return out.reshape(cz, tb, 2, 2 * k).transpose(1, 2, 0, 3)[:, None]


def solution(mesh):
    in_specs = (
        P(None, "tile", None, None, "chan"),
        P(("tile", "beam"), None, None, "chan"),
        P(("tile", "beam")),
        P(None, "tile"),
        P("beam"),
        P(),
    )
    out_specs = P("tile", "beam", None, "chan", None)
    return jax.shard_map(
        functools.partial(body, mesh), mesh=mesh, in_specs=in_specs, out_specs=out_specs, check_vma=False
    )
```

time: 85 us -> 39.1 us (0.46); the launches traced: 83.6 us -> 38.9 us
  waiting for transfers between devices: 27.4 us -> 0 us
  Pallas kernels: 0 us -> 20.3 us
  other arithmetic: 19.3 us -> 0 us
  between operations: 14.9 us -> 0.68 us
  local copies, waits for them, and re-layouts: 8.27 us -> 17.9 us
  blocking collectives: 8.47 us -> 0 us
  starting transfers between devices: 4.81 us -> 0 us
    reduce_scatter x1 -> x0, waiting for transfers between devices: 22.9 us -> none  [body(): return lax.psum_scatter(streams, 'tile', scatter_dimension=0, tiled=True)]
    pallas_call x0 -> x1, Pallas kernels: none -> 20.3 us  [body(): pl.pallas_call(functools.partial(kernel, cfg), out_shape=jax.ShapeDtypeSt...]
    reduce_sum x1 -> x0, other arithmetic: 10.5 us -> none  [body(): jnp.sum(weight_re[None] * volt_re - weight_im[None] * volt_im, axis=2)]
    transpose x0 -> x2, local copies, waits for them, and re-layouts: none -> 9.83 us  [rows_of(): return jnp.swapaxes(split, -3, -2).reshape(-1, LANES)]
    reshape x0 -> x3, local copies, waits for them, and re-layouts: none -> 5.37 us  [the longest x2 3.93 us: rows_of(): split = array.reshape(lead + (2, width // LANES, LANES))]
    all_to_all x1 -> x0, starting transfers between devices: 4.81 us -> none  [body(): lax.all_to_all(partial_value.reshape(partial_value.shape[:4] + (fine_loca...]
    convert_element_type x1 -> x0, other arithmetic: 4.52 us -> none  [body(): block = voltages.astype(jnp.float32)]
    all_to_all x1 -> x0, waiting for transfers between devices: 4.47 us -> none  [body(): lax.all_to_all(partial_value.reshape(partial_value.shape[:4] + (fine_loca...]
  transfers between devices with their start and end apart: 2 -> 0, of which waited for: 2 -> 0; matrix products, arithmetic and copies ran while one was open for 1% -> 0% of each run, Pallas kernels for 0% -> 0%
where the time goes in v1:
time: 39.1 us; the launch traced here: 38.9 us
  Pallas kernels  20.3 us (52%)
  local copies, waits for them, and re-layouts  17.9 us (46%)
  between operations  0.68 us (2%)
    pallas_call x1, Pallas kernels, body(): pl.pallas_call(functools.partial(kernel, cfg), out_shape=jax.ShapeDtypeSt...  20.3 us
    transpose x2, local copies, waits for them, and re-layouts, rows_of(): return jnp.swapaxes(split, -3, -2).reshape(-1, LANES)  9.83 us
    reshape x2, local copies, waits for them, and re-layouts, rows_of(): split = array.reshape(lead + (2, width // LANES, LANES))  3.93 us
    unnamed x4, local copies, waits for them, and re-layouts  2.69 us
    reshape x1, local copies, waits for them, and re-layouts, body(): return out.reshape(cz, tb, 2, 2 * k).transpose(1, 2, 0, 3)[:, None]  1.44 us

profile of v1, /device:TPU:1, one launch (start us, length us, event | category | flops | bytes accessed | tf_op | source)
XLA Modules:
  0.0 38.9 jit_solution(1088517152629353103)
XLA Ops:
  0.0 2.7 %copy.14 = bf16[32,32,2,2,384]{4,1,3,2,0:T(8,128)(2,1)S(1)} copy(bf16[32,32,2,2,384]{4,3,2,1,0:T(2,128)(2,1)} %param.10) | data formatting | bytes 6291456 | tf_op args[0]
  2.7 3.9 %reshape.15 = bf16[32,32,2,2,3,128]{5,4,1,3,2,0:T(4,128)(2,1)} reshape(bf16[32,32,2,2,384]{4,1,3,2,0:T(8,128)(2,1)S(1)} %copy.14) | data formatting | bytes 6291456 | tf_op jit(solution)/shard_map/reshape | solution.py:390
  6.6 0.0 copy-start
  6.6 9.1 %copy.15 = bf16[32,32,2,3,2,128]{5,4,3,2,1,0:T(2,128)(2,1)} copy(bf16[32,32,2,3,2,128]{5,3,1,4,2,0:T(4,128)(2,1)} %bitcast.19) | data formatting | bytes 6291456 | tf_op jit(solution)/shard_map/transpose | solution.py:391
  15.7 0.0 copy-done
  15.8 0.7 %copy.17 = f32[16,2,3,2,128]{4,3,2,1,0:T(2,128)} copy(f32[16,2,3,2,128]{4,2,0,3,1:T(4,128)S(1)} %bitcast.21) | data formatting | bytes 196608 | tf_op jit(solution)/shard_map/transpose | solution.py:391
  17.1 20.3 %shard_map.100 = f32[3,8,512]{2,1,0:T(8,128)} custom-call(bf16[12288,128]{1,0:T(8,128)(2,1)} %bitcast.20, f32[192,128]{1,0:T(8,128)} %bitcast.22, s32[16]{0:T(128)} %flag_ref.1, f32[32,64]{1,0:T(8,128)} %bitcast.24, s32[1]{0:T(128)S(6)} %copy.21.point_ref, f32[12,128]{1,0:T(8,128)} %synth_ref.1, f32[24,128]{1,0:T(8,128)} %constant.8.clone.chan_ref, ...), custom_call_target="tpu_custom_call" | custom-call | tf_op jit(solution)/shard_map/pallas_call | solution.py:420
  37.5 1.4 %copy.20 = f32[3,8,2,256]{3,2,0,1:T(2,128)} copy(f32[3,8,2,256]{3,1,2,0:T(8,128)} %bitcast.23) | data formatting | bytes 98304 | tf_op jit(solution)/shard_map/reshape | solution.py:460
  (2 shorter events, 0.0 us)
Async XLA Ops:
  6.6 9.1 %copy-start = (f32[16,2,2,384]{3,2,1,0:T(2,128)S(1)}, f32[16,2,2,384]{3,2,1,0:T(2,128)}, u32[]{:S(2)}) copy-start(f32[16,2,2,384]{3,2,1,0:T(2,128)} %param.11) | copy-start | bytes 294916

commit v2 on v1

--- a/solution.py
+++ b/solution.py
@@ -79,6 +79,7 @@
     dftl_ref,
     out_ref,
     volt,
+    own_gain,
     gains,
     w_re,
     w_im,
@@ -92,6 +93,7 @@
     dft_l,
     volt_sem,
     table_sem,
+    own_sem,
     gain_send,
     gain_recv,
     part_send,
@@ -103,24 +105,38 @@
     tile = lax.axis_index("tile")
     chan = lax.axis_index("chan")
     beam = lax.axis_index("beam")
-    rows_t = n_all * 4 * cz
-    rows_n = 4 * cz
+    rows_t = n_all * 4
+    held_t = n_all * 2
 
     def peer(t, z, b):
         return {"tile": t, "chan": z, "beam": b}
 
     order = sorted(range(1, nt), key=lambda d: abs(2 * d - nt)) + [0]
+    own_loads = [
+        pltpu.make_async_copy(
+            gain_ref.at[:, :, pl.ds(c * LANES, LANES)], own_gain.at[c], own_sem.at[c]
+        )
+        for c in range(cz)
+    ]
+    for load in own_loads:
+        load.start()
     loads = []
     for slot, d in enumerate(order):
         block = lax.rem(tile + d, nt)
         loads.append(
-            pltpu.make_async_copy(
-                volt_ref.at[pl.ds(pl.multiple_of(block * (tb * rows_t), 16), tb * rows_t)],
-                volt.at[slot],
-                volt_sem.at[slot],
-            )
+            [
+                pltpu.make_async_copy(
+                    volt_ref.at[pl.ds(block * (tb * held_t), tb * held_t), :, pl.ds(c * LANES, LANES)],
+                    volt.at[slot, c],
+                    volt_sem.at[slot, c],
+                )
+                for c in range(cz)
+            ]
         )
-    loads[0].start()
+    for load in loads[0]:
+        load.start()
+    volt_rows = volt.reshape(nt, cz, tb * rows_t, LANES)
+    own_rows = own_gain.reshape(cz, own_gain.shape[1] * 2, LANES)
 
     barrier = pltpu.get_barrier_semaphore()
     count = 0
@@ -140,8 +156,9 @@
         )
         count += 1
 
-    for load in loads[1:]:
-        load.start()
+    for group in loads[1:]:
+        for load in group:
+            load.start()
     tables = [
         pltpu.make_async_copy(dfth_ref, dft_h, table_sem.at[0]),
         pltpu.make_async_copy(dftl_ref, dft_l, table_sem.at[1]),
@@ -149,18 +166,23 @@
     for copy in tables:
         copy.start()
 
-    pair = 2 * rows_n
-    row = lax.broadcasted_iota(jnp.int32, (pair, LANES), 0)
-    first = row < rows_n
-    even = lax.rem(row, 2) == 0
+    row = lax.broadcasted_iota(jnp.int32, (8, LANES), 0)
+    first = row < 4
+    even = lax.rem(lax.broadcasted_iota(jnp.int32, (rows_t, LANES), 0), 2) == 0
     n_own = n_all // nb
 
+    for load in own_loads:
+        load.wait()
     if exchange:
-        for i in range(n_own // 2):
-            use = jnp.where(
-                first, flag_ref[2 * i].astype(F32), flag_ref[2 * i + 1].astype(F32)
-            )
-            gains[beam, pl.ds(i * pair, pair), :] = use * gain_ref[pl.ds(i * pair, pair), :]
+        use = jnp.concatenate(
+            [
+                jnp.where(first, flag_ref[2 * i].astype(F32), flag_ref[2 * i + 1].astype(F32))
+                for i in range(n_own // 2)
+            ],
+            axis=0,
+        )
+        for c in range(cz):
+            gains[beam, c] = use * own_rows[c]
 
     for h in range(1, halo + 1):
 
@@ -187,64 +209,60 @@
     select = lax.broadcasted_iota(jnp.int32, delay_ref.shape, 1) == point_ref[0]
     delay = jnp.sum(jnp.where(select, delay_ref[...], 0.0), axis=1, keepdims=True)
     delay = jnp.broadcast_to(delay, (n_all, LANES))
-    frequency = (chan_ref[...] + (chan * fz).astype(F32) + 0.5) / (COARSE * nz * fz)
-
-    def phase(i):
-        cycles = (
+    delay = jnp.concatenate(
+        [
             jnp.where(
                 first,
-                jnp.broadcast_to(delay[2 * i : 2 * i + 1], (pair, LANES)),
-                jnp.broadcast_to(delay[2 * i + 1 : 2 * i + 2], (pair, LANES)),
+                jnp.broadcast_to(delay[2 * i : 2 * i + 1], (8, LANES)),
+                jnp.broadcast_to(delay[2 * i + 1 : 2 * i + 2], (8, LANES)),
             )
-            * frequency
-        )
+            for i in range(n_all // 2)
+        ],
+        axis=0,
+    )
+    for c in range(cz):
+        frequency = (chan_ref[pl.ds(c, 1), :] + (chan * fz).astype(F32) + 0.5) / (COARSE * nz * fz)
+        cycles = delay * frequency
         turn = cycles - jnp.floor(cycles + 0.5)
         square = turn * turn
-        return horner(COS_COEF, square), turn * horner(SIN_COEF, square)
-
-    for i in range(n_all // 2):
-        cosine, sine = phase(i)
-        w_re[pl.ds(i * pair, pair), :] = cosine
-        w_im[pl.ds(i * pair, pair), :] = sine
+        w_re[c] = horner(COS_COEF, square)
+        w_im[c] = turn * horner(SIN_COEF, square)
 
     for copy in gain_copies:
         copy.wait_recv()
 
-    for i in range(n_all // 2):
+    for c in range(cz):
         if exchange:
-            owner, inner = divmod(2 * i, n_own)
-            gain = gains[owner, pl.ds(inner * rows_n, pair), :]
+            gain = jnp.concatenate([gains[b, c] for b in range(nb)], axis=0)
         else:
-            gain = gain_ref[pl.ds(i * pair, pair), :]
-        cosine = w_re[pl.ds(i * pair, pair), :]
-        sine = w_im[pl.ds(i * pair, pair), :]
-        swapped = jnp.where(
-            even, pltpu.roll(gain, pair - 1, 0), -pltpu.roll(gain, 1, 0)
-        )
-        weight = gain * cosine + swapped * sine
-        w_re[pl.ds(i * pair, pair), :] = jnp.where(even, weight, pltpu.roll(weight, 1, 0))
-        w_im[pl.ds(i * pair, pair), :] = jnp.where(even, pltpu.roll(weight, pair - 1, 0), weight)
-
-    quad = 2 * pair
+            gain = own_rows[c]
+        swapped = jnp.where(even, pltpu.roll(gain, rows_t - 1, 0), -pltpu.roll(gain, 1, 0))
+        weight = gain * w_re[c] + swapped * w_im[c]
+        w_re[c] = jnp.where(even, weight, pltpu.roll(weight, 1, 0))
+        w_im[c] = jnp.where(even, pltpu.roll(weight, rows_t - 1, 0), weight)
+
     unroll = 2
+    kept = cz * 2 * 8
     part_copies = []
     for slot, d in enumerate(order):
-        loads[slot].wait()
+        for load in loads[slot]:
+            load.wait()
 
         def step(s, carry):
-            sums = [[jnp.zeros((quad, LANES), F32)] * 2 for _ in range(unroll)]
-            for q in range(n_all // 4):
-                wr = w_re[pl.ds(q * quad, quad), :]
-                wi = w_im[pl.ds(q * quad, quad), :]
+            for c in range(cz):
+                sums = [[jnp.zeros((16, LANES), F32)] * 2 for _ in range(unroll)]
+                for q in range(rows_t // 16):
+                    wr = w_re[c, pl.ds(q * 16, 16), :]
+                    wi = w_im[c, pl.ds(q * 16, 16), :]
+                    for u in range(unroll):
+                        begin = pl.multiple_of((s * unroll + u) * rows_t, 16) + q * 16
+                        v = volt_rows[slot, c, pl.ds(begin, 16), :].astype(F32)
+                        sums[u] = [sums[u][0] + wr * v, sums[u][1] + wi * v]
                 for u in range(unroll):
-                    begin = pl.multiple_of((s * unroll + u) * rows_t, 16) + q * quad
-                    v = volt[slot, pl.ds(begin, quad), :].astype(F32)
-                    sums[u] = [sums[u][0] + wr * v, sums[u][1] + wi * v]
-            for u in range(unroll):
-                begin = pl.multiple_of((s * unroll + u) * quad, 8)
-                for which in range(2):
-                    value = sums[u][which]
-                    acc[slot % 2, pl.ds(begin + which * pair, pair), :] = value[:pair] + value[pair:]
+                    begin = pl.multiple_of((s * unroll + u) * kept, 8)
+                    for which in range(2):
+                        value = sums[u][which]
+                        acc[slot % 2, pl.ds(begin + (c * 2 + which) * 8, 8), :] = value[:8] + value[8:]
             return carry
 
         lax.fori_loop(0, tb // unroll, step, 0)
@@ -252,8 +270,8 @@
         def take(which, p, c, ri):
             total = None
             for half in range(2):
-                start = which * pair + half * rows_n + (p * cz + c) * 2 + ri
-                value = acc[slot % 2, pl.ds(start, tb, stride=quad), :]
+                start = (c * 2 + which) * 8 + half * 4 + p * 2 + ri
+                value = acc[slot % 2, pl.ds(start, tb, stride=kept), :]
                 total = value if total is None else total + value
             return total
 
@@ -385,12 +403,6 @@
                     pack_copy(h, dz).wait_send()
 
 
-def rows_of(array):
-    lead, width = array.shape[:-2], array.shape[-1]
-    split = array.reshape(lead + (2, width // LANES, LANES))
-    return jnp.swapaxes(split, -3, -2).reshape(-1, LANES)
-
-
 def body(mesh, voltages, calib_gain, tile_flags, delays, pointing, synth_filter):
     nt, nz, nb = mesh.shape["tile"], mesh.shape["chan"], mesh.shape["beam"]
     total_rows, n_all = voltages.shape[:2]
@@ -406,9 +418,7 @@
     if not exchange:
         gain = gain * tile_flags.astype(F32)[:, None, None, None]
         gain = lax.all_gather(gain, "beam", axis=0, tiled=True)
-    rows_n = 4 * cz
-    r = np.arange(2 * rows_n)[:, None] % rows_n % (2 * cz) // 2
-    local = r * LANES + np.arange(LANES)[None, :]
+    local = np.arange(width).reshape(-1, LANES)
     channel = (local % COARSE * k + local // COARSE).astype(np.float32)
     dft_h, dft_l = dft_table(nz, fz)
     cfg = (nt, nz, nb, tb, n_all, taps, fz, cz, halo, exchange)
@@ -420,14 +430,15 @@
     out = pl.pallas_call(
         functools.partial(kernel, cfg),
         out_shape=jax.ShapeDtypeStruct((cz, tb, 4 * k), F32),
-        in_specs=[anywhere, vmem, smem, vmem, smem, vmem, vmem, vmem, anywhere, anywhere],
+        in_specs=[anywhere, anywhere, smem, vmem, smem, vmem, vmem, vmem, anywhere, anywhere],
         out_specs=vmem,
         scratch_shapes=[
-            pltpu.VMEM((nt, tb * n_all * rows_n, LANES), BF16),
-            pltpu.VMEM((nb, n_own * rows_n, LANES), F32),
-            pltpu.VMEM((n_all * rows_n, LANES), F32),
-            pltpu.VMEM((n_all * rows_n, LANES), F32),
-            pltpu.VMEM((2, tb * 4 * rows_n, LANES), F32),
+            pltpu.VMEM((nt, cz, tb * n_all * 2, 2, LANES), BF16),
+            pltpu.VMEM((cz, gain.shape[0] * 2, 2, LANES), F32),
+            pltpu.VMEM((nb, cz, n_own * 4, LANES), F32),
+            pltpu.VMEM((cz, n_all * 4, LANES), F32),
+            pltpu.VMEM((cz, n_all * 4, LANES), F32),
+            pltpu.VMEM((2, tb * cz * 16, LANES), F32),
             pltpu.VMEM((nt, 4 * cz, tb, LANES), F32),
             pltpu.VMEM((nt - 1, 4 * cz, tb, LANES), F32),
             pltpu.VMEM((nz, cz, tb, LANES), F32),
@@ -435,8 +446,9 @@
             pltpu.VMEM((cz * span, 4 * k), F32),
             pltpu.VMEM(dft_h.shape, BF16),
             pltpu.VMEM(dft_l.shape, BF16),
-            dma((nt,)),
+            dma((nt, cz)),
             dma((2,)),
+            dma((cz,)),
             dma((max(nb - 1, 1),)),
             dma((max(nb - 1, 1),)),
             dma((nt,)),
@@ -446,8 +458,8 @@
         ],
         compiler_params=pltpu.CompilerParams(collective_id=0, has_side_effects=True),
     )(
-        rows_of(voltages),
-        rows_of(gain),
+        voltages.reshape(-1, 2, width),
+        gain.reshape(-1, 2, width),
         tile_flags,
         delays.T,
         pointing,

time: 39.1 us -> 23.1 us (0.59)
  local copies, waits for them, and re-layouts: 17.9 us -> 1.44 us
    transpose x2 -> x0, local copies, waits for them, and re-layouts: 9.83 us -> none  [rows_of(): return jnp.swapaxes(split, -3, -2).reshape(-1, LANES)]
    reshape x2 -> x0, local copies, waits for them, and re-layouts: 3.93 us -> none  [rows_of(): split = array.reshape(lead + (2, width // LANES, LANES))]
    unnamed x4 -> x0, local copies, waits for them, and re-layouts: 2.69 us -> none
where the time goes in v2:
time: 23.1 us; the launch traced here: 22.7 us
  Pallas kernels  20.6 us (89%)
  local copies, waits for them, and re-layouts  1.44 us (6%)
  between operations  0.66 us (3%)
    pallas_call x1, Pallas kernels, body(): pl.pallas_call(functools.partial(kernel, cfg), out_shape=jax.ShapeDtypeSt...  20.6 us
    reshape x1, local copies, waits for them, and re-layouts, body(): return out.reshape(cz, tb, 2, 2 * k).transpose(1, 2, 0, 3)[:, None]  1.44 us

profile of v2, /device:TPU:1, one launch (start us, length us, event | category | flops | bytes accessed | tf_op | source)
XLA Modules:
  0.0 22.7 jit_solution(13091433342694005826)
XLA Ops:
  0.7 20.6 %shard_map.100 = f32[3,8,512]{2,1,0:T(8,128)} custom-call(bf16[2048,2,384]{2,1,0:T(2,128)(2,1)} %bitcast.9, f32[32,2,384]{2,1,0:T(2,128)} %bitcast.11, s32[16]{0:T(128)} %flag_ref.1, f32[32,64]{1,0:T(8,128)} %bitcast.12, s32[1]{0:T(128)S(6)} %copy.14.point_ref, f32[12,128]{1,0:T(8,128)} %synth_ref.1, f32[3,128]{1,0:T(4,128)} %constant.8.clone.chan_ref, ...), custom_call_target="tpu_custom_call" | custom-call | tf_op jit(solution)/shard_map/pallas_call | solution.py:430
  21.2 1.4 %copy.13 = f32[3,8,2,256]{3,2,0,1:T(2,128)} copy(f32[3,8,2,256]{3,1,2,0:T(8,128)} %bitcast.10) | data formatting | bytes 98304 | tf_op jit(solution)/shard_map/reshape | solution.py:472

commit v3 on v2

--- a/solution.py
+++ b/solution.py
@@ -69,15 +69,22 @@
     cfg,
     volt_ref,
     gain_ref,
+    flag_src,
+    delay_src,
+    point_src,
+    synth_src,
+    chan_src,
+    perm_src,
+    dfth_ref,
+    dftl_ref,
+    out_ref,
     flag_ref,
     delay_ref,
     point_ref,
     synth_ref,
     chan_ref,
     perm_ref,
-    dfth_ref,
-    dftl_ref,
-    out_ref,
+    small_sem,
     volt,
     own_gain,
     gains,
@@ -112,13 +119,44 @@
         return {"tile": t, "chan": z, "beam": b}
 
     order = sorted(range(1, nt), key=lambda d: abs(2 * d - nt)) + [0]
+    barrier = pltpu.get_barrier_semaphore()
+    count = 0
+    for dt in range(nt):
+        for dz in range(nz):
+            if dt or dz:
+                pl.semaphore_signal(
+                    barrier,
+                    inc=1,
+                    device_id=peer(lax.rem(tile + dt, nt), lax.rem(chan + dz, nz), beam),
+                    device_id_type=MESH,
+                )
+                count += 1
+    for db in range(1, nb):
+        pl.semaphore_signal(
+            barrier, inc=1, device_id=peer(tile, chan, lax.rem(beam + db, nb)), device_id_type=MESH
+        )
+        count += 1
+
+    small = [
+        pltpu.make_async_copy(src, dst, small_sem.at[i])
+        for i, (src, dst) in enumerate(
+            [
+                (flag_src, flag_ref),
+                (point_src, point_ref),
+                (delay_src, delay_ref),
+                (chan_src, chan_ref),
+                (synth_src, synth_ref),
+                (perm_src, perm_ref),
+            ]
+        )
+    ]
     own_loads = [
         pltpu.make_async_copy(
             gain_ref.at[:, :, pl.ds(c * LANES, LANES)], own_gain.at[c], own_sem.at[c]
         )
         for c in range(cz)
     ]
-    for load in own_loads:
+    for load in own_loads + small[:4]:
         load.start()
     loads = []
     for slot, d in enumerate(order):
@@ -138,24 +176,6 @@
     volt_rows = volt.reshape(nt, cz, tb * rows_t, LANES)
     own_rows = own_gain.reshape(cz, own_gain.shape[1] * 2, LANES)
 
-    barrier = pltpu.get_barrier_semaphore()
-    count = 0
-    for dt in range(nt):
-        for dz in range(nz):
-            if dt or dz:
-                pl.semaphore_signal(
-                    barrier,
-                    inc=1,
-                    device_id=peer(lax.rem(tile + dt, nt), lax.rem(chan + dz, nz), beam),
-                    device_id_type=MESH,
-                )
-                count += 1
-    for db in range(1, nb):
-        pl.semaphore_signal(
-            barrier, inc=1, device_id=peer(tile, chan, lax.rem(beam + db, nb)), device_id_type=MESH
-        )
-        count += 1
-
     for group in loads[1:]:
         for load in group:
             load.start()
@@ -163,7 +183,7 @@
         pltpu.make_async_copy(dfth_ref, dft_h, table_sem.at[0]),
         pltpu.make_async_copy(dftl_ref, dft_l, table_sem.at[1]),
     ]
-    for copy in tables:
+    for copy in small[4:] + tables:
         copy.start()
 
     row = lax.broadcasted_iota(jnp.int32, (8, LANES), 0)
@@ -171,7 +191,7 @@
     even = lax.rem(lax.broadcasted_iota(jnp.int32, (rows_t, LANES), 0), 2) == 0
     n_own = n_all // nb
 
-    for load in own_loads:
+    for load in own_loads + small[:1]:
         load.wait()
     if exchange:
         use = jnp.concatenate(
@@ -206,6 +226,8 @@
             copy.start()
             gain_copies.append(copy)
 
+    for copy in small[1:4]:
+        copy.wait()
     select = lax.broadcasted_iota(jnp.int32, delay_ref.shape, 1) == point_ref[0]
     delay = jnp.sum(jnp.where(select, delay_ref[...], 0.0), axis=1, keepdims=True)
     delay = jnp.broadcast_to(delay, (n_all, LANES))
@@ -305,6 +327,8 @@
     )
     high = sums.astype(BF16)
     low = (sums - high.astype(F32)).astype(BF16)
+    for copy in small[4:]:
+        copy.wait()
     table = perm_ref[...]
     moved = jnp.dot(high, table, preferred_element_type=F32) + jnp.dot(
         low, table, preferred_element_type=F32
@@ -421,18 +445,25 @@
     local = np.arange(width).reshape(-1, LANES)
     channel = (local % COARSE * k + local // COARSE).astype(np.float32)
     dft_h, dft_l = dft_table(nz, fz)
+    perm = gather_table(nz, fz, cz)
     cfg = (nt, nz, nb, tb, n_all, taps, fz, cz, halo, exchange)
     vmem = pl.BlockSpec(memory_space=pltpu.VMEM)
-    smem = pl.BlockSpec(memory_space=pltpu.SMEM)
     anywhere = pl.BlockSpec(memory_space=pl.ANY)
     span = (halo + 1) * tb
     dma = pltpu.SemaphoreType.DMA
     out = pl.pallas_call(
         functools.partial(kernel, cfg),
         out_shape=jax.ShapeDtypeStruct((cz, tb, 4 * k), F32),
-        in_specs=[anywhere, anywhere, smem, vmem, smem, vmem, vmem, vmem, anywhere, anywhere],
+        in_specs=[anywhere] * 10,
         out_specs=vmem,
         scratch_shapes=[
+            pltpu.SMEM(tile_flags.shape, jnp.int32),
+            pltpu.VMEM(delays.shape[::-1], F32),
+            pltpu.SMEM(pointing.shape, jnp.int32),
+            pltpu.VMEM(synth_filter.shape, F32),
+            pltpu.VMEM(channel.shape, F32),
+            pltpu.VMEM(perm.shape, BF16),
+            dma((6,)),
             pltpu.VMEM((nt, cz, tb * n_all * 2, 2, LANES), BF16),
             pltpu.VMEM((cz, gain.shape[0] * 2, 2, LANES), F32),
             pltpu.VMEM((nb, cz, n_own * 4, LANES), F32),
@@ -465,7 +496,7 @@
         pointing,
         synth_filter,
         jnp.asarray(channel),
-        jnp.asarray(gather_table(nz, fz, cz)),
+        jnp.asarray(perm),
         jnp.asarray(dft_h),
         jnp.asarray(dft_l),
     )

time: 23.1 us -> 22.2 us (0.961)
  Pallas kernels: 20.6 us -> 19.8 us
    pallas_call x1, Pallas kernels: 20.6 us -> 19.8 us  [body(): pl.pallas_call(functools.partial(kernel, cfg), out_shape=jax.ShapeDtypeSt...]
where the time goes in v3:
time: 22.2 us; the launch traced here: 21.9 us
  Pallas kernels  19.8 us (89%)
  local copies, waits for them, and re-layouts  1.44 us (6%)
  between operations  0.66 us (3%)
    pallas_call x1, Pallas kernels, body(): pl.pallas_call(functools.partial(kernel, cfg), out_shape=jax.ShapeDtypeSt...  19.8 us
    reshape x1, local copies, waits for them, and re-layouts, body(): return out.reshape(cz, tb, 2, 2 * k).transpose(1, 2, 0, 3)[:, None]  1.44 us

profile of v3, /device:TPU:1, one launch (start us, length us, event | category | flops | bytes accessed | tf_op | source)
XLA Modules:
  0.0 21.9 jit_solution(13091556547223824927)
XLA Ops:
  0.7 19.8 %shard_map.100 = f32[3,8,512]{2,1,0:T(8,128)} custom-call(bf16[2048,2,384]{2,1,0:T(2,128)(2,1)} %bitcast.9, f32[32,2,384]{2,1,0:T(2,128)} %bitcast.11, s32[16]{0:T(128)} %flag_src.1, f32[32,64]{1,0:T(8,128)} %bitcast.12, s32[1]{0:T(128)S(6)} %copy.14.point_src, f32[12,128]{1,0:T(8,128)} %synth_src.1, f32[3,128]{1,0:T(4,128)} %constant.8.clone.chan_src, ...), custom_call_target="tpu_custom_call" | custom-call | tf_op jit(solution)/shard_map/pallas_call | solution.py:454
  20.4 1.4 %copy.13 = f32[3,8,2,256]{3,2,0,1:T(2,128)} copy(f32[3,8,2,256]{3,1,2,0:T(8,128)} %bitcast.10) | data formatting | bytes 98304 | tf_op jit(solution)/shard_map/reshape | solution.py:503

commit v4 on v3

--- a/solution.py
+++ b/solution.py
@@ -188,8 +188,9 @@
 
     row = lax.broadcasted_iota(jnp.int32, (8, LANES), 0)
     first = row < 4
-    even = lax.rem(lax.broadcasted_iota(jnp.int32, (rows_t, LANES), 0), 2) == 0
     n_own = n_all // nb
+    share = n_own * 4 if exchange else rows_t
+    even = lax.rem(lax.broadcasted_iota(jnp.int32, (share, LANES), 0), 2) == 0
 
     for load in own_loads + small[:1]:
         load.wait()
@@ -250,50 +251,70 @@
         w_re[c] = horner(COS_COEF, square)
         w_im[c] = turn * horner(SIN_COEF, square)
 
-    for copy in gain_copies:
-        copy.wait_recv()
-
-    for c in range(cz):
-        if exchange:
-            gain = jnp.concatenate([gains[b, c] for b in range(nb)], axis=0)
-        else:
-            gain = own_rows[c]
-        swapped = jnp.where(even, pltpu.roll(gain, rows_t - 1, 0), -pltpu.roll(gain, 1, 0))
-        weight = gain * w_re[c] + swapped * w_im[c]
-        w_re[c] = jnp.where(even, weight, pltpu.roll(weight, 1, 0))
-        w_im[c] = jnp.where(even, pltpu.roll(weight, rows_t - 1, 0), weight)
+    def weigh(start, gain_of):
+        rows = pl.ds(start, share)
+        for c in range(cz):
+            gain = gain_of(c)
+            swapped = jnp.where(even, pltpu.roll(gain, share - 1, 0), -pltpu.roll(gain, 1, 0))
+            weight = gain * w_re[c, rows, :] + swapped * w_im[c, rows, :]
+            w_re[c, rows, :] = jnp.where(even, weight, pltpu.roll(weight, 1, 0))
+            w_im[c, rows, :] = jnp.where(even, pltpu.roll(weight, share - 1, 0), weight)
 
     unroll = 2
     kept = cz * 2 * 8
-    part_copies = []
-    for slot, d in enumerate(order):
-        for load in loads[slot]:
-            load.wait()
-
+
+    def accumulate(slot, starts, extend):
         def step(s, carry):
             for c in range(cz):
                 sums = [[jnp.zeros((16, LANES), F32)] * 2 for _ in range(unroll)]
-                for q in range(rows_t // 16):
-                    wr = w_re[c, pl.ds(q * 16, 16), :]
-                    wi = w_im[c, pl.ds(q * 16, 16), :]
-                    for u in range(unroll):
-                        begin = pl.multiple_of((s * unroll + u) * rows_t, 16) + q * 16
-                        v = volt_rows[slot, c, pl.ds(begin, 16), :].astype(F32)
-                        sums[u] = [sums[u][0] + wr * v, sums[u][1] + wi * v]
+                for start in starts:
+                    for q in range(share // 16):
+                        at = start + q * 16
+                        wr = w_re[c, pl.ds(at, 16), :]
+                        wi = w_im[c, pl.ds(at, 16), :]
+                        for u in range(unroll):
+                            begin = pl.multiple_of((s * unroll + u) * rows_t + at, 16)
+                            v = volt_rows[slot, c, pl.ds(begin, 16), :].astype(F32)
+                            sums[u] = [sums[u][0] + wr * v, sums[u][1] + wi * v]
                 for u in range(unroll):
                     begin = pl.multiple_of((s * unroll + u) * kept, 8)
                     for which in range(2):
                         value = sums[u][which]
-                        acc[slot % 2, pl.ds(begin + (c * 2 + which) * 8, 8), :] = value[:8] + value[8:]
+                        value = value[:8] + value[8:]
+                        rows = pl.ds(begin + (c * 2 + which) * 8, 8)
+                        acc[slot, rows, :] = acc[slot, rows, :] + value if extend else value
             return carry
 
         lax.fori_loop(0, tb // unroll, step, 0)
+
+    starts = [0]
+    if exchange:
+        starts = [pl.multiple_of(lax.rem(beam + db, nb) * share, 16) for db in range(nb)]
+        weigh(starts[0], lambda c: gains[beam, c])
+        for slot in range(nt):
+            for load in loads[slot]:
+                load.wait()
+            accumulate(slot, starts[:1], False)
+        for copy in gain_copies:
+            copy.wait_recv()
+        for db in range(1, nb):
+            weigh(starts[db], lambda c, db=db: gains[lax.rem(beam + db, nb), c])
+    else:
+        weigh(0, lambda c: own_rows[c])
+    part_copies = []
+    for slot, d in enumerate(order):
+        if exchange:
+            accumulate(slot, starts[1:], True)
+        else:
+            for load in loads[slot]:
+                load.wait()
+            accumulate(slot, starts, False)
 
         def take(which, p, c, ri):
             total = None
             for half in range(2):
                 start = (c * 2 + which) * 8 + half * 4 + p * 2 + ri
-                value = acc[slot % 2, pl.ds(start, tb, stride=kept), :]
+                value = acc[slot, pl.ds(start, tb, stride=kept), :]
                 total = value if total is None else total + value
             return total
 
@@ -437,7 +458,7 @@
     cz = COARSE // nz
     halo = -(-(taps - 1) // tb)
     n_own = calib_gain.shape[0]
-    exchange = n_own % 2 == 0
+    exchange = n_own % 4 == 0 and mesh.shape["beam"] > 1
     gain = calib_gain
     if not exchange:
         gain = gain * tile_flags.astype(F32)[:, None, None, None]
@@ -469,7 +490,7 @@
             pltpu.VMEM((nb, cz, n_own * 4, LANES), F32),
             pltpu.VMEM((cz, n_all * 4, LANES), F32),
             pltpu.VMEM((cz, n_all * 4, LANES), F32),
-            pltpu.VMEM((2, tb * cz * 16, LANES), F32),
+            pltpu.VMEM((nt, tb * cz * 16, LANES), F32),
             pltpu.VMEM((nt, 4 * cz, tb, LANES), F32),
             pltpu.VMEM((nt - 1, 4 * cz, tb, LANES), F32),
             pltpu.VMEM((nz, cz, tb, LANES), F32),

time: 22.2 us -> 21.9 us (0.986)
  Pallas kernels: 19.8 us -> 19.5 us
    pallas_call x1, Pallas kernels: 19.8 us -> 19.5 us  [body(): pl.pallas_call(functools.partial(kernel, cfg), out_shape=jax.ShapeDtypeSt...]
where the time goes in v4:
time: 21.9 us; the launch traced here: 21.6 us
  Pallas kernels  19.5 us (89%)
  local copies, waits for them, and re-layouts  1.44 us (7%)
  between operations  0.66 us (3%)
    pallas_call x1, Pallas kernels, body(): pl.pallas_call(functools.partial(kernel, cfg), out_shape=jax.ShapeDtypeSt...  19.5 us
    reshape x1, local copies, waits for them, and re-layouts, body(): return out.reshape(cz, tb, 2, 2 * k).transpose(1, 2, 0, 3)[:, None]  1.44 us

profile of v4, /device:TPU:1, one launch (start us, length us, event | category | flops | bytes accessed | tf_op | source)
XLA Modules:
  0.0 21.6 jit_solution(18421567386395242997)
XLA Ops:
  0.7 19.5 %shard_map.100 = f32[3,8,512]{2,1,0:T(8,128)} custom-call(bf16[2048,2,384]{2,1,0:T(2,128)(2,1)} %bitcast.9, f32[32,2,384]{2,1,0:T(2,128)} %bitcast.11, s32[16]{0:T(128)} %flag_src.1, f32[32,64]{1,0:T(8,128)} %bitcast.12, s32[1]{0:T(128)S(6)} %copy.14.point_src, f32[12,128]{1,0:T(8,128)} %synth_src.1, f32[3,128]{1,0:T(4,128)} %constant.8.clone.chan_src, ...), custom_call_target="tpu_custom_call" | custom-call | tf_op jit(solution)/shard_map/pallas_call | solution.py:475
  20.2 1.4 %copy.13 = f32[3,8,2,256]{3,2,0,1:T(2,128)} copy(f32[3,8,2,256]{3,1,2,0:T(8,128)} %bitcast.10) | data formatting | bytes 98304 | tf_op jit(solution)/shard_map/reshape | solution.py:524
